TPU v7x, 128 devices: a whole 4x4x4 slice. The times are simulated.
128 devices in a mesh: fsdp: 16 (over x_lo, y, core), expert: 8 (over x_hi, z).
Axes of the slice: x: 4 (x_hi: 2, x_lo: 2; x = x_hi * 2 + x_lo), y: 4, z: 4, core: 2. Of those that a mesh axis runs over, the one named last changes fastest.
Arguments:
- pool: bfloat16 [256, 128, 4096], P('fsdp', None, 'expert'), may hold values from -6 to 6
- picks: int32 [16, 8], P('fsdp'), may hold values from 0 to 15, as said below
- lengths: int32 [256], P('fsdp'), may hold values from 1 to 128
- routes: int32 [16384, 2], P(('fsdp', 'expert')), may hold values from 0 to 7, all different within a row; in each aligned block of 128 rows (0 to 127, 128 to 255, ...) at most 64 rows name the same one
- route_gap: float32 [16384], P(('fsdp', 'expert')), may hold values from -8 to 8
- gate_weight: bfloat16 [8, 14336, 4096], P('expert', 'fsdp'), may hold values from -0.09375 to 0.09375
- down_weight: bfloat16 [8, 14336, 4096], P('expert', 'fsdp'), may hold values from -0.046875 to 0.046875
Outputs:
- moe_out: bfloat16 [16384, 4096], P(('fsdp', 'expert'))
Inputs may be any that keep to these rules, and one draw needn't show every extreme that they name: `picks`: each row holds 8 different candidate numbers. `routes`: the two experts of a token differ; among the 128 tokens of one window no expert is named by more than 64 tokens.
All inputs are finite; a program needn't handle non-finite values.
Results may differ from a plain program's by a relative error of at most 0.019.
Values may be sent and summed in bfloat16 or wider, within the bound.
A program may use at most 128 MiB of HBM per device.

v0:
```python
import jax
import jax.numpy as jnp
from jax import lax
from jax.sharding import PartitionSpec as P

EXPERTS = 8
TOP = 2
CAP = 14


def sent_to_all(value, axis):
    length = lax.axis_size(axis)
    return lax.all_to_all(
        jnp.broadcast_to(value[None], (length, *value.shape)), axis, 0, 0, tiled=True
    )


def laid_out(tiles, dim):
    shape = list(tiles.shape[1:])
    shape[dim] *= tiles.shape[0]
    return jnp.moveaxis(tiles, 0, dim).reshape(shape)


def collect(value, axis, dim):
    tiles = sent_to_all(value, axis)
    return laid_out(tiles, dim)


def slot_targets(block_routes, length):
    row_count = block_routes.shape[0]
    is_live = jnp.arange(row_count, dtype=jnp.int32) < length
    expert_ids = jnp.concatenate([block_routes[:, 0], block_routes[:, 1]])
    live_both = jnp.concatenate([is_live, is_live])
    expert_hits = (
        (expert_ids[:, None] == jnp.arange(EXPERTS, dtype=jnp.int32)[None, :]) & live_both[:, None]
    ).astype(jnp.int32)
    earlier = jnp.cumsum(expert_hits, axis=0) - expert_hits
    slot_rank = jnp.sum(earlier * expert_hits, axis=1)
    is_kept = live_both & (slot_rank < CAP)
    return jnp.where(is_kept, expert_ids * CAP + slot_rank, -1)


def dispatch_table(targets):
    row_count = targets.shape[0] // 2
    slot_ids = jnp.arange(EXPERTS * CAP, dtype=jnp.int32)[:, None]
    return (
        (slot_ids == targets[None, :row_count]) | (slot_ids == targets[None, row_count:])
    ).astype(jnp.bfloat16)


def combine_table(targets, gap_row):
    row_count = targets.shape[0] // 2
    slot_ids = jnp.arange(EXPERTS * CAP, dtype=jnp.int32)[None, :]
    weight_first = jax.nn.sigmoid(gap_row)[:, None]
    weight_second = jax.nn.sigmoid(-gap_row)[:, None]
    first_hit = (targets[:row_count, None] == slot_ids).astype(jnp.float32)
    second_hit = (targets[row_count:, None] == slot_ids).astype(jnp.float32)
    return first_hit * weight_first + second_hit * weight_second


def local(pool, picks, lengths, routes, route_gap, gate_weight, down_weight):
    expert_count = lax.axis_size("expert")
    expert_local = gate_weight.shape[0]
    window_rows = pool.shape[1]
    model_width = gate_weight.shape[2]
    my_column = lax.axis_index("expert")
    chosen = picks[0]
    selected = jnp.take(pool, chosen, axis=0)
    chosen_len = jnp.take(lengths, chosen)
    column_routes = collect(routes, "expert", 0)
    all_targets = jax.vmap(slot_targets)(
        column_routes.reshape(expert_count, window_rows, TOP), chosen_len
    )
    tables = jax.vmap(dispatch_table)(all_targets)
    outgoing = jnp.einsum(
        "bsp,bpd->bsd", tables, selected, preferred_element_type=jnp.float32
    ).astype(jnp.bfloat16)
    outgoing = outgoing.reshape(expert_count, expert_count, expert_local, CAP, selected.shape[2])
    arrived = lax.all_to_all(outgoing, "expert", split_axis=1, concat_axis=4, tiled=True)
    arrived = arrived.reshape(expert_count, expert_local, CAP, model_width)
    my_targets = lax.dynamic_index_in_dim(all_targets, my_column, 0, keepdims=False)
    gate_act = jnp.einsum(
        "fbecd,ehd->fbech",
        lax.all_gather(arrived[None], "fsdp", axis=0, tiled=True),
        gate_weight,
        preferred_element_type=jnp.float32,
    )
    hidden = jax.nn.silu(gate_act).astype(jnp.bfloat16)
    dev_rows = expert_count * expert_local * CAP
    partial_value = jnp.einsum(
        "fbech,ehd->fbecd", hidden, down_weight, preferred_element_type=jnp.float32
    )
    summed = lax.psum_scatter(
        partial_value.reshape(dev_rows * lax.axis_size("fsdp"), model_width).astype(jnp.bfloat16),
        "fsdp",
        scatter_dimension=0,
        tiled=True,
    )
    expert_out = summed.reshape(expert_count, expert_local, CAP, model_width)
    returned = lax.all_to_all(expert_out, "expert", split_axis=0, concat_axis=1, tiled=True)
    flat_out = returned.reshape(EXPERTS * CAP, model_width).astype(jnp.float32)
    combine = combine_table(my_targets, route_gap)
    mixed = jnp.dot(combine, flat_out, preferred_element_type=jnp.float32)
    return mixed.astype(jnp.bfloat16)


def solution(mesh):
    placed = (
        P("fsdp", None, "expert"),
        P("fsdp", None),
        P("fsdp"),
        P(("fsdp", "expert"), None),
        P(("fsdp", "expert")),
        P("expert", "fsdp", None),
        P("expert", "fsdp", None),
    )
    return jax.shard_map(
        local, mesh=mesh, in_specs=placed, out_specs=P(("fsdp", "expert"), None), check_vma=False
    )
```

profile of v0, /device:TPU:0, one launch (start us, length us, event | category | flops | bytes accessed | tf_op | source)
XLA Modules:
  0.0 329.3 jit_solution(543143658603108437)
XLA Ops:
  6.5 1.4 broadcast_in_dim.17
  8.0 7.9 %all-to-all-start = ((s32[8,128,2]{1,2,0:T(2,128)}), s32[8,128,2]{1,2,0:T(2,128)S(1)}, u32[]{:S(2)}, u32[]{:S(2)}) async-start(s32[8,128,2]{1,2,0:T(2,128)} %broadcast_in_dim.17), calls=%async_computation | async-start | bytes 16384 | tf_op jit(solution)/shard_map/all_to_all | solution.py:13
  15.9 0.7 fusion.35
  16.6 1.3 gather_fusion
  17.9 0.7 broadcast_select_fusion
  18.5 0.1 iota_compare_fusion.10
  18.6 0.1 iota_compare_fusion.9
  18.7 0.6 gather_fusion.1
  19.3 4.2 %all-to-all-done = s32[8,128,2]{1,2,0:T(2,128)S(1)} async-done(((s32[8,128,2]{1,2,0:T(2,128)}), s32[8,128,2]{1,2,0:T(2,128)S(1)}, u32[]{:S(2)}, u32[]{:S(2)}) %all-to-all-start) | async-done | bytes 8224 | tf_op jit(solution)/shard_map/all_to_all | solution.py:13
  23.6 4.5 %reduce-window.6 = s32[8,8,2,128]{3,1,2,0:T(8,128)S(1)} reduce-window(s32[8,8,2,128]{3,1,2,0:T(8,128)S(1)} %fusion.27, s32[]{:T(128)} %constant.36.clone.1), window={size=1x1x1x128 pad=0_0x0_0x0_0x127_0}, to_apply=%region_0.1 | reduce-window | flops 2080768 | bytes 131076 | tf_op jit(solution)/shard_map/reduce-window
  28.1 0.1 slice.40
  28.2 0.2 copy.28
  28.4 0.1 fusion.33
  28.5 0.1 fusion.21
  28.6 0.5 convolution_convert_fusion.1
  29.1 0.5 copy.30
  29.6 18.0 %all_to_all.29 = bf16[8,8,1,14,512]{4,0,3,2,1:T(8,128)(2,1)S(1)} all-to-all(bf16[8,8,1,14,512]{4,0,3,2,1:T(8,128)(2,1)S(1)} %bitcast.91), channel_id=1, replica_groups=mesh['fsdp'=16,'expert'=8] {'expert'}, dimensions={1} | all-to-all | bytes 1835008 | tf_op jit(solution)/shard_map/all_to_all | solution.py:79
  47.6 0.5 copy.32
  48.1 1.3 broadcast_in_dim_reshape.3
  49.5 0.2 reduce-scatter.2.cloned.1.call-start
  49.7 78.9 %all-gather.2.cloned.1.call-done = bf16[16,8,1,14,4096]{4,1,3,2,0:T(8,128)(2,1)} async-done(((bf16[1,8,1,14,4096]{4,1,3,2,0:T(8,128)(2,1)}), bf16[16,8,1,14,4096]{4,1,3,2,0:T(8,128)(2,1)}) %all-gather.2.cloned.1.call-update) | async-done | bytes 14680080 | tf_op jit(solution)/shard_map/all_gather | solution.py:84
  128.6 20.7 %fusion.7 = bf16[16,8,1,14,896]{4,1,3,0,2:T(8,128)(2,1)S(1)} fusion(bf16[1,896,4096]{2,1,0:T(8,128)(2,1)} %param.12, bf16[16,8,1,14,4096]{4,1,3,2,0:T(8,128)(2,1)} %all-gather.2.cloned.1.call-done), kind=kOutput, calls=%fused_computation.12 | convolution fusion | flops 13161365504 | bytes 25231360 | tf_op jit(solution)/shard_map/fbecd,ehd->fbech/dot_general | solution.py:82
  149.4 20.9 %convert_bitcast_fusion = bf16[16,8,1,14,4096]{4,1,3,0,2:T(8,128)(2,1)} fusion(bf16[1,896,4096]{2,1,0:T(8,128)(2,1)} %param.13, bf16[16,8,1,14,896]{4,1,3,0,2:T(8,128)(2,1)S(1)} %fusion.7), kind=kOutput, calls=%fused_computation.4 | convolution fusion | flops 13160677376 | bytes 25231360 | tf_op jit(solution)/shard_map/fbech,ehd->fbecd/dot_general | solution.py:90
  170.3 17.5 %copy.33 = bf16[16,8,1,14,4096]{4,3,1,0,2:T(8,128)(2,1)} copy(bf16[16,8,1,14,4096]{4,1,3,0,2:T(8,128)(2,1)} %convert_bitcast_fusion) | data formatting | bytes 29360128 | tf_op jit(solution)/shard_map/convert_element_type | solution.py:94
  187.7 18.0 %convert_element_type.43 = bf16[1792,4096]{1,0:T(8,128)(2,1)} reshape(bf16[16,8,1,14,4096]{4,3,1,0,2:T(8,128)(2,1)} %copy.33) | data formatting | bytes 29360128 | tf_op jit(solution)/shard_map/convert_element_type | solution.py:94
  205.8 90.1 %reduce-scatter.2.cloned.1.call-done = bf16[112,4096]{1,0:T(8,128)(2,1)} async-done(((bf16[1792,4096]{1,0:T(8,128)(2,1)}), bf16[112,4096]{1,0:T(8,128)(2,1)}) %reduce-scatter.2.cloned.1.call-update) | async-done | bytes 917520 | tf_op jit(solution)/shard_map/reduce_scatter | solution.py:93
  295.9 2.4 reshape.152
  298.3 6.8 %all-to-all-start.2 = ((bf16[8,1,14,4096]{3,2,1,0:T(8,128)(2,1)}), bf16[8,1,14,4096]{3,2,1,0:T(8,128)(2,1)S(1)}, u32[]{:S(2)}, u32[]{:S(2)}) async-start(bf16[8,1,14,4096]{3,2,1,0:T(8,128)(2,1)} %bitcast.90), calls=%async_computation.3 | async-start | bytes 2097152 | tf_op jit(solution)/shard_map/all_to_all | solution.py:100
  305.1 0.1 dynamic-slice_bitcast_fusion.1
  305.2 13.4 %all-to-all-done.2 = bf16[8,1,14,4096]{3,2,1,0:T(8,128)(2,1)S(1)} async-done(((bf16[8,1,14,4096]{3,2,1,0:T(8,128)(2,1)}), bf16[8,1,14,4096]{3,2,1,0:T(8,128)(2,1)S(1)}, u32[]{:S(2)}, u32[]{:S(2)}) %all-to-all-start.2) | async-done | bytes 917536 | tf_op jit(solution)/shard_map/all_to_all | solution.py:100
  318.6 1.2 reshape.153
  319.8 2.7 convolution_convert_fusion
  (22 shorter events, 0.2 us)
Async XLA Ops:
  6.5 12.2 %copy-start = (bf16[16,128,512]{2,1,0:T(8,128)(2,1)S(1)}, bf16[16,128,512]{2,1,0:T(8,128)(2,1)}, u32[]{:S(2)}) copy-start(bf16[16,128,512]{2,1,0:T(8,128)(2,1)} %param.7) | copy-start | bytes 6291460
  8.0 15.6 %all-to-all-start = ((s32[8,128,2]{1,2,0:T(2,128)}), s32[8,128,2]{1,2,0:T(2,128)S(1)}, u32[]{:S(2)}, u32[]{:S(2)}) async-start(s32[8,128,2]{1,2,0:T(2,128)} %broadcast_in_dim.17), calls=%async_computation | async-start | bytes 16384 | tf_op jit(solution)/shard_map/all_to_all | solution.py:13
  15.9 112.8 %all-gather.2.cloned.1.call-start = ((), (), s32[]{:S(2)}) async-start(), calls=%async_computation.4 | async-start | bytes 15597568 | tf_op jit(solution)/shard_map/all_gather | solution.py:84
  49.5 246.4 %reduce-scatter.2.cloned.1.call-start = ((), (), s32[]{:S(2)}) async-start(), calls=%async_computation.5 | async-start | bytes 15597568 | tf_op jit(solution)/shard_map/reduce_scatter | solution.py:93
  205.8 99.3 %copy-start.2 = (f32[128]{0:T(128)S(1)}, f32[128]{0:T(128)}, u32[]{:S(2)}) copy-start(f32[128]{0:T(128)} %param.11) | copy-start | bytes 1540
  205.8 116.7 %copy-start.1 = (bf16[16,128,512]{2,1,0:T(8,128)(2,1)S(1)}, bf16[16,128,512]{2,1,0:T(8,128)(2,1)}, u32[]{:S(2)}) copy-start(bf16[16,128,512]{2,1,0:T(8,128)(2,1)} %param.7) | copy-start | bytes 6291460
  298.3 20.3 %all-to-all-start.2 = ((bf16[8,1,14,4096]{3,2,1,0:T(8,128)(2,1)}), bf16[8,1,14,4096]{3,2,1,0:T(8,128)(2,1)S(1)}, u32[]{:S(2)}, u32[]{:S(2)}) async-start(bf16[8,1,14,4096]{3,2,1,0:T(8,128)(2,1)} %bitcast.90), calls=%async_computation.3 | async-start | bytes 2097152 | tf_op jit(solution)/shard_map/all_to_all | solution.py:100
Sparse Core Ops, SparseCore 0:
  49.6 78.9 all-gather.1
  205.9 89.9 reduce-scatter.1
where the time goes:
time: 330 us; the launch traced here: 329 us
  waiting for transfers between devices  187 us (57%)
  local copies, waits for them, and re-layouts  45.2 us (14%)
  matrix products  44.8 us (14%)
  blocking collectives  18 us (5%)
  starting transfers between devices  14.9 us (5%)
  between operations  13.6 us (4%)
  other arithmetic  6.23 us (2%)
    reduce_scatter x1, waiting for transfers between devices, local(): lax.psum_scatter(partial_value.reshape(dev_rows * lax.axis_size('fsdp'),...  90.1 us
    all_gather x1, waiting for transfers between devices, local(): lax.all_gather(arrived[None], 'fsdp', axis=0, tiled=True)  78.9 us
    convert_element_type x2, local copies, waits for them, and re-layouts, local(): partial_value.reshape(dev_rows * lax.axis_size('fsdp'), model_width)  35.5 us
    dot_general x1, matrix products, local(): jnp.einsum('fbech,ehd->fbecd', hidden, down_weight, preferred_element_typ...  20.9 us
    dot_general x1, matrix products, local(): jnp.einsum('fbecd,ehd->fbech', lax.all_gather(arrived[None], 'fsdp', axis...  20.7 us
    all_to_all x1, blocking collectives, local(): lax.all_to_all(outgoing, 'expert', split_axis=1, concat_axis=4, tiled=True)  18 us
    all_to_all x1, waiting for transfers between devices, local(): lax.all_to_all(expert_out, 'expert', split_axis=0, concat_axis=1, tiled=T...  13.4 us
    all_to_all x1, starting transfers between devices, sent_to_all(): lax.all_to_all(jnp.broadcast_to(value[None], (length, *value.shape)), axi...  7.89 us
  transfers between devices with their start and end apart: 4, of which 4 were waited for; matrix products, arithmetic and copies ran while one was open for 1% of the time, Pallas kernels for 0%

commit v1 on v0

--- a/solution.py
+++ b/solution.py
@@ -6,6 +6,11 @@
 EXPERTS = 8
 TOP = 2
 CAP = 14
+
+
+def all_by_exchange(shard, name, along):
+    sent = jnp.stack([shard] * lax.axis_size(name))
+    return jnp.concatenate(lax.all_to_all(sent, name, 0, 0), axis=along)
 
 
 def sent_to_all(value, axis):
@@ -81,7 +86,7 @@
     my_targets = lax.dynamic_index_in_dim(all_targets, my_column, 0, keepdims=False)
     gate_act = jnp.einsum(
         "fbecd,ehd->fbech",
-        lax.all_gather(arrived[None], "fsdp", axis=0, tiled=True),
+        all_by_exchange(arrived[None], "fsdp", 0),
         gate_weight,
         preferred_element_type=jnp.float32,
     )

time: 330 us -> 420 us (1.27)
  blocking collectives: 18 us -> 187 us
  waiting for transfers between devices: 187 us -> 102 us
  local copies, waits for them, and re-layouts: 45.2 us -> 51.3 us
    all_to_all x0 -> x1, blocking collectives: none -> 169 us  [all_by_exchange(): return jnp.concatenate(lax.all_to_all(sent, name, 0, 0), axis=along)]
    all_gather x1 -> x0, waiting for transfers between devices: 78.9 us -> none  [local(): lax.all_gather(arrived[None], 'fsdp', axis=0, tiled=True)]
    reduce_scatter x1, waiting for transfers between devices: 90.1 us -> 83.9 us  [local(): lax.psum_scatter(partial_value.reshape(dev_rows * lax.axis_size('fsdp'),...]
    another operation x3 -> x4, local copies, waits for them, and re-layouts: 1.35 us -> 7.44 us  [the longest x2 7.43 us: all_by_exchange(): sent = jnp.stack([shard] * lax.axis_size(name))]
  transfers between devices with their start and end apart: 4 -> 3, of which waited for: 4 -> 3; matrix products, arithmetic and copies ran while one was open for 1% -> 1% of each run, Pallas kernels for 0% -> 0%
where the time goes in v1:
time: 420 us; the launch traced here: 419 us
  blocking collectives  187 us (45%)
  waiting for transfers between devices  102 us (24%)
  local copies, waits for them, and re-layouts  51.3 us (12%)
  matrix products  44.8 us (11%)
  starting transfers between devices  15 us (4%)
  between operations  13.6 us (3%)
  other arithmetic  6.23 us (1%)
    all_to_all x1, blocking collectives, all_by_exchange(): return jnp.concatenate(lax.all_to_all(sent, name, 0, 0), axis=along)  169 us
    reduce_scatter x1, waiting for transfers between devices, local(): lax.psum_scatter(partial_value.reshape(dev_rows * lax.axis_size('fsdp'),...  83.9 us
    convert_element_type x2, local copies, waits for them, and re-layouts, local(): partial_value.reshape(dev_rows * lax.axis_size('fsdp'), model_width)  35.5 us
    dot_general x1, matrix products, local(): jnp.einsum('fbecd,ehd->fbech', all_by_exchange(arrived[None], 'fsdp', 0),...  21.8 us
    dot_general x1, matrix products, local(): jnp.einsum('fbech,ehd->fbecd', hidden, down_weight, preferred_element_typ...  19.8 us
    all_to_all x1, blocking collectives, local(): lax.all_to_all(outgoing, 'expert', split_axis=1, concat_axis=4, tiled=True)  18 us
    all_to_all x1, waiting for transfers between devices, local(): lax.all_to_all(expert_out, 'expert', split_axis=0, concat_axis=1, tiled=T...  13.4 us
  transfers between devices with their start and end apart: 3, of which 3 were waited for; matrix products, arithmetic and copies ran while one was open for 1% of the time, Pallas kernels for 0%

profile of v1, /device:TPU:0, one launch (start us, length us, event | category | flops | bytes accessed | tf_op | source)
XLA Modules:
  0.0 419.0 jit_solution(9792713057598010121)
XLA Ops:
  6.5 1.4 broadcast_in_dim.17
  8.0 7.9 %all-to-all-start = ((s32[8,128,2]{1,2,0:T(2,128)}), s32[8,128,2]{1,2,0:T(2,128)S(1)}, u32[]{:S(2)}, u32[]{:S(2)}) async-start(s32[8,128,2]{1,2,0:T(2,128)} %broadcast_in_dim.17), calls=%async_computation | async-start | bytes 16384 | tf_op jit(solution)/shard_map/all_to_all | solution.py:18
  15.9 0.7 fusion.35
  16.6 1.3 gather_fusion
  17.9 0.7 broadcast_select_fusion
  18.5 0.1 iota_compare_fusion.10
  18.6 0.1 iota_compare_fusion.9
  18.7 0.6 gather_fusion.1
  19.3 4.2 %all-to-all-done = s32[8,128,2]{1,2,0:T(2,128)S(1)} async-done(((s32[8,128,2]{1,2,0:T(2,128)}), s32[8,128,2]{1,2,0:T(2,128)S(1)}, u32[]{:S(2)}, u32[]{:S(2)}) %all-to-all-start) | async-done | bytes 8224 | tf_op jit(solution)/shard_map/all_to_all | solution.py:18
  23.6 4.5 %reduce-window.6 = s32[8,8,2,128]{3,1,2,0:T(8,128)S(1)} reduce-window(s32[8,8,2,128]{3,1,2,0:T(8,128)S(1)} %fusion.27, s32[]{:T(128)} %constant.36.clone.1), window={size=1x1x1x128 pad=0_0x0_0x0_0x127_0}, to_apply=%region_0.1 | reduce-window | flops 2080768 | bytes 131076 | tf_op jit(solution)/shard_map/reduce-window
  28.1 0.1 slice.40
  28.2 0.2 copy.19
  28.4 0.1 fusion.33
  28.5 0.1 fusion.21
  28.6 0.5 convolution_convert_fusion.1
  29.1 0.5 copy.21
  29.6 18.0 %all_to_all.34 = bf16[8,8,1,14,512]{4,0,3,2,1:T(8,128)(2,1)S(1)} all-to-all(bf16[8,8,1,14,512]{4,0,3,2,1:T(8,128)(2,1)S(1)} %bitcast.91), channel_id=1, replica_groups=mesh['fsdp'=16,'expert'=8] {'expert'}, dimensions={1} | all-to-all | bytes 1835008 | tf_op jit(solution)/shard_map/all_to_all | solution.py:84
  47.6 0.5 copy.23
  48.1 0.4 stack_broadcast_in_dim_reshape.2
  48.5 7.0 %stack.3 = bf16[16,1,8,1,14,4096]{5,2,4,3,1,0:T(8,128)(2,1)} broadcast(bf16[8,14,4096]{2,0,1:T(8,128)(2,1)S(1)} %stack_broadcast_in_dim_reshape.2), dimensions={2,4,5} | broadcast | bytes 15597568 | tf_op jit(solution)/shard_map/stack | solution.py:12
  55.6 168.6 %all_to_all.35 = bf16[16,1,8,1,14,4096]{5,2,4,3,1,0:T(8,128)(2,1)} all-to-all(bf16[16,1,8,1,14,4096]{5,2,4,3,1,0:T(8,128)(2,1)} %stack.3), channel_id=1, replica_groups=mesh['fsdp'=16,'expert'=8] {'fsdp'}, dimensions={0} | all-to-all | bytes 29360128 | tf_op jit(solution)/shard_map/all_to_all | solution.py:13
  224.2 21.8 %fusion.7 = bf16[16,8,1,14,896]{4,1,3,0,2:T(8,128)(2,1)} fusion(bf16[1,896,4096]{2,1,0:T(8,128)(2,1)} %param.12, bf16[16,1,8,1,14,4096]{5,2,4,3,1,0:T(8,128)(2,1)} %all_to_all.35), kind=kOutput, calls=%fused_computation.12 | convolution fusion | flops 13161365504 | bytes 25231360 | tf_op jit(solution)/shard_map/fbecd,ehd->fbech/dot_general | solution.py:87
  246.0 19.8 %convert_bitcast_fusion = bf16[16,8,1,14,4096]{4,1,3,0,2:T(8,128)(2,1)} fusion(bf16[1,896,4096]{2,1,0:T(8,128)(2,1)S(1)} %bitcast.100, bf16[16,8,1,14,896]{4,1,3,0,2:T(8,128)(2,1)} %fusion.7), kind=kOutput, calls=%fused_computation.4 | convolution fusion | flops 13160677376 | bytes 25231360 | tf_op jit(solution)/shard_map/fbech,ehd->fbecd/dot_general | solution.py:95
  265.8 17.5 %copy.24 = bf16[16,8,1,14,4096]{4,3,1,0,2:T(8,128)(2,1)} copy(bf16[16,8,1,14,4096]{4,1,3,0,2:T(8,128)(2,1)} %convert_bitcast_fusion) | data formatting | bytes 29360128 | tf_op jit(solution)/shard_map/convert_element_type | solution.py:99
  283.3 18.0 %convert_element_type.43 = bf16[1792,4096]{1,0:T(8,128)(2,1)} reshape(bf16[16,8,1,14,4096]{4,3,1,0,2:T(8,128)(2,1)} %copy.24) | data formatting | bytes 29360128 | tf_op jit(solution)/shard_map/convert_element_type | solution.py:99
  301.3 83.9 %reduce-scatter.2.cloned.1.call-done = bf16[112,4096]{1,0:T(8,128)(2,1)} async-done(((bf16[1792,4096]{1,0:T(8,128)(2,1)}), bf16[112,4096]{1,0:T(8,128)(2,1)}) %reduce-scatter.2.cloned.1.call-update) | async-done | bytes 917520 | tf_op jit(solution)/shard_map/reduce_scatter | solution.py:98
  385.3 2.4 reshape.158
  387.7 7.1 %all-to-all-start.3 = ((bf16[8,1,14,4096]{3,2,1,0:T(8,128)(2,1)}), bf16[8,1,14,4096]{3,2,1,0:T(8,128)(2,1)S(1)}, u32[]{:S(2)}, u32[]{:S(2)}) async-start(bf16[8,1,14,4096]{3,2,1,0:T(8,128)(2,1)} %bitcast.90), calls=%async_computation.4 | async-start | bytes 2097152 | tf_op jit(solution)/shard_map/all_to_all | solution.py:105
  394.8 0.1 dynamic-slice_bitcast_fusion.1
  394.9 13.4 %all-to-all-done.3 = bf16[8,1,14,4096]{3,2,1,0:T(8,128)(2,1)S(1)} async-done(((bf16[8,1,14,4096]{3,2,1,0:T(8,128)(2,1)}), bf16[8,1,14,4096]{3,2,1,0:T(8,128)(2,1)S(1)}, u32[]{:S(2)}, u32[]{:S(2)}) %all-to-all-start.3) | async-done | bytes 917536 | tf_op jit(solution)/shard_map/all_to_all | solution.py:105
  408.3 1.2 reshape.159
  409.5 2.7 convolution_convert_fusion
  (26 shorter events, 0.2 us)
Async XLA Ops:
  6.5 12.2 %copy-start = (bf16[16,128,512]{2,1,0:T(8,128)(2,1)S(1)}, bf16[16,128,512]{2,1,0:T(8,128)(2,1)}, u32[]{:S(2)}) copy-start(bf16[16,128,512]{2,1,0:T(8,128)(2,1)} %param.7) | copy-start | bytes 6291460
  8.0 15.6 %all-to-all-start = ((s32[8,128,2]{1,2,0:T(2,128)}), s32[8,128,2]{1,2,0:T(2,128)S(1)}, u32[]{:S(2)}, u32[]{:S(2)}) async-start(s32[8,128,2]{1,2,0:T(2,128)} %broadcast_in_dim.17), calls=%async_computation | async-start | bytes 16384 | tf_op jit(solution)/shard_map/all_to_all | solution.py:18
  15.9 369.4 %reduce-scatter.2.cloned.1.call-start = ((), (), s32[]{:S(2)}) async-start(), calls=%async_computation.5 | async-start | bytes 15597568 | tf_op jit(solution)/shard_map/reduce_scatter | solution.py:98
  55.6 190.4 %slice-start = ((s8[7340032]{0:T(1024)(128)(4,1)}), s8[4194304]{0:T(1024)(128)(4,1)S(1)}, s32[]{:S(2)}) async-start(s8[7340032]{0:T(1024)(128)(4,1)} %bitcast.99), calls=%async_computation.6 | async-start | bytes 8388608
  224.2 21.8 %slice-start.1 = ((s8[7340032]{0:T(1024)(128)(4,1)}), s8[3145728]{0:T(1024)(128)(4,1)S(1)}, s32[]{:S(2)}) async-start(s8[7340032]{0:T(1024)(128)(4,1)} %bitcast.99), calls=%async_computation.7 | async-start | bytes 6291456
  301.3 93.5 %copy-start.2 = (f32[128]{0:T(128)S(1)}, f32[128]{0:T(128)}, u32[]{:S(2)}) copy-start(f32[128]{0:T(128)} %param.11) | copy-start | bytes 1540
  301.3 110.8 %copy-start.1 = (bf16[16,128,512]{2,1,0:T(8,128)(2,1)S(1)}, bf16[16,128,512]{2,1,0:T(8,128)(2,1)}, u32[]{:S(2)}) copy-start(bf16[16,128,512]{2,1,0:T(8,128)(2,1)} %param.7) | copy-start | bytes 6291460
  387.7 20.6 %all-to-all-start.3 = ((bf16[8,1,14,4096]{3,2,1,0:T(8,128)(2,1)}), bf16[8,1,14,4096]{3,2,1,0:T(8,128)(2,1)S(1)}, u32[]{:S(2)}, u32[]{:S(2)}) async-start(bf16[8,1,14,4096]{3,2,1,0:T(8,128)(2,1)} %bitcast.90), calls=%async_computation.4 | async-start | bytes 2097152 | tf_op jit(solution)/shard_map/all_to_all | solution.py:105
Sparse Core Ops, SparseCore 0:
  301.4 83.7 reduce-scatter.1
